TPU v7x, 128 devices: a whole 4x4x4 slice. The times are simulated.
128 devices in a mesh: lat: 16 (over z_hi, y_lo, x), lon: 4 (over z_lo, core), lev: 2 (over y_hi).
Axes of the slice: x: 4, y: 4 (y_hi: 2, y_lo: 2; y = y_hi * 2 + y_lo), z: 4 (z_hi: 2, z_lo: 2; z = z_hi * 2 + z_lo), core: 2. Of those that a mesh axis runs over, the one named last changes fastest.
Arguments:
- field_values: float32 [64, 256, 192, 128], P('lat', 'lon', 'lev'), may hold values from 0.2 to 1.8
- crowding: float32 [64, 256, 192, 128], P('lat', 'lon', 'lev'), may hold values from 0.5 to 2
Outputs:
- field_values_end: float32 [64, 256, 192, 128], P('lat', 'lon', 'lev')
All inputs are finite; a program needn't handle non-finite values.
Results may differ from a plain program's by a relative error of at most 0.00002.
Values sent between devices are 32-bit elements; how exact they have to be, the bound alone decides.
A program may use at most 384 MiB of HBM per device.

v0:
```python
import jax
import jax.numpy as jnp
from jax import lax
from jax.sharding import PartitionSpec as P

STEPS = 3


def with_halo(x, sides, width):
    edges = {}
    for axis, dim in sides:
        size, length = (lax.axis_size(axis), x.shape[dim])
        up = [(i, (i + 1) % size) for i in range(size)]
        last = lax.slice_in_dim(x, length - width, length, axis=dim)
        first = lax.slice_in_dim(x, 0, width, axis=dim)
        edges[dim] = (
            lax.ppermute(last, axis, up),
            lax.ppermute(first, axis, [(b, a) for a, b in up]),
        )
    done = []
    for _, dim in sides:
        low, high = edges[dim]
        around = [(width, width) if d in done else (0, 0) for d in range(x.ndim)]
        x = jnp.concatenate([jnp.pad(low, around), x, jnp.pad(high, around)], axis=dim)
        done.append(dim)
    return x


def without_rim(values, dims):
    for dim in dims:
        values = lax.slice_in_dim(values, 1, values.shape[dim] - 1, axis=dim)
    return values


def shifted_cells(values, dim, start, dims):
    others = [other for other in dims if other != dim]
    values = without_rim(values, others)
    return lax.slice_in_dim(values, start, start + values.shape[dim] - 2, axis=dim)


def march_step(padded, crowding):
    middle = without_rim(padded, (0, 1, 2))
    lower = [shifted_cells(padded, dim, 0, (0, 1, 2)) for dim in (0, 1, 2)]
    upper = [shifted_cells(padded, dim, 2, (0, 1, 2)) for dim in (0, 1, 2)]
    spread = lower[0] + upper[0] + lower[1] + upper[1] + lower[2] + upper[2] - 6.0 * middle
    return middle + 0.1 * spread + 0.2 * middle * (1.0 - middle * crowding)


def local(field_values, crowding):
    for step in range(STEPS):
        padded = with_halo(field_values, (("lat", 0), ("lon", 1), ("lev", 2)), 1)
        field_values = march_step(padded, crowding)
    return field_values


def solution(mesh):
    placed = (P("lat", "lon", "lev", None), P("lat", "lon", "lev", None))
    return jax.shard_map(
        local, mesh=mesh, in_specs=placed, out_specs=P("lat", "lon", "lev", None), check_vma=False
    )
```

profile of v0, /device:TPU:16, one launch (start us, length us, event | category | flops | bytes accessed | tf_op | source)
XLA Modules:
  0.0 409.5 jit_solution(11875402927914270513)
XLA Ops:
  0.0 5.0 %fusion.41 = (f32[1,64,96,128]{3,2,1,0:T(8,128)}, f32[1,64,96,128]{3,2,1,0:T(8,128)S(1)}) fusion(f32[4,64,96,128]{3,2,1,0:T(8,128)} %param.2), kind=kLoop, calls=%fused_computation.92 | loop fusion | bytes 12582912 | tf_op jit(solution)/shard_map/slice | solution.py:15
  5.0 1.5 collective-permute-start
  6.4 5.3 %collective-permute-start.1 = (f32[1,64,96,128]{3,2,1,0:T(8,128)}, f32[1,64,96,128]{3,2,1,0:T(8,128)S(1)}, u32[]{:S(2)}, u32[]{:S(2)}) collective-permute-start(f32[1,64,96,128]{3,2,1,0:T(8,128)} %get-tuple-element.21), channel_id=1, source_target_pairs={{8,0},{16,8},{24,16},{32,24},{40,32},{48,40},{56,48},{64,56},{72,6... | collective-permute-start | bytes 9437192 | tf_op jit(solution)/shard_map/ppermute | solution.py:18
  11.7 1.0 fusion.40
  12.9 1.7 collective-permute-start.3
  14.6 2.4 fusion.39
  17.7 67.1 %collective-permute-done.2 = f32[4,1,96,128]{3,2,1,0:T(8,128)S(1)} collective-permute-done((f32[4,1,96,128]{3,2,1,0:T(8,128)S(1)}, f32[4,1,96,128]{3,2,1,0:T(8,128)S(1)}, u32[]{:S(2)}, u32[]{:S(2)}) %collective-permute-start.2) | collective-permute-done | bytes 196640 | tf_op jit(solution)/shard_map/ppermute | solution.py:17
  85.9 1.8 constant_dynamic-update-slice_fusion.2
  87.7 10.3 %constant_dynamic-update-slice_fusion.1 = f32[6,64,96,128]{3,2,1,0:T(8,128)} fusion(f32[6,64,96,128]{3,2,1,0:T(8,128)} %constant_dynamic-update-slice_fusion.2, f32[4,64,96,128]{3,2,1,0:T(8,128)} %param.2), kind=kLoop, calls=%fused_computation.82 | loop fusion | bytes 25165824
  98.1 1.7 copy-done
  99.8 1.9 constant_dynamic-update-slice_fusion
  101.7 41.2 %fusion.27 = f32[4,64,96,128]{3,2,1,0:T(8,128)} fusion(f32[4,64,96,128]{3,2,1,0:T(8,128)} %param.2, f32[4,64,1,128]{3,2,1,0:T(1,128)} %bitcast.11, f32[6,1,96,128]{3,2,1,0:T(8,128)} %pad.39, f32[6,64,96,128]{3,2,1,0:T(8,128)} %constant_dynamic-update-slice_fusion, f32[6,1,96,128]{3,2,1,0:T(8,128)S(1)} %pad.38, f32[4,64,1,128]{3,2,1,0:T(1,128)} %bitcast.9, ...), kind=kLoop, calls=%fused_computation.64 | loop fusion | flops 94371840 | bytes 63766528 | tf_op jit(solution)/shard_map/add | solution.py:46
  142.9 3.3 fusion.37
  146.2 6.5 %collective-permute-start.7 = (f32[1,64,96,128]{3,2,1,0:T(8,128)S(1)}, f32[1,64,96,128]{3,2,1,0:T(8,128)S(1)}, u32[]{:S(2)}, u32[]{:S(2)}) collective-permute-start(f32[1,64,96,128]{3,2,1,0:T(8,128)S(1)} %get-tuple-element.14), channel_id=1, source_target_pairs={{8,0},{16,8},{24,16},{32,24},{40,32},{48,40},{56,48},{64,56},{72,6... | collective-permute-start | bytes 9437192 | tf_op jit(solution)/shard_map/ppermute | solution.py:18
  153.9 1.7 collective-permute-start.9
  155.6 1.7 fusion.36
  157.4 3.3 collective-permute-start.10
  160.6 61.3 %collective-permute-done.8 = f32[4,1,96,128]{3,2,1,0:T(8,128)S(1)} collective-permute-done((f32[4,1,96,128]{3,2,1,0:T(8,128)S(1)}, f32[4,1,96,128]{3,2,1,0:T(8,128)S(1)}, u32[]{:S(2)}, u32[]{:S(2)}) %collective-permute-start.8) | collective-permute-done | bytes 196640 | tf_op jit(solution)/shard_map/ppermute | solution.py:17
  222.0 2.6 collective-permute-start.11
  225.3 3.6 collective-permute-done.11
  228.9 1.7 copy-done.2
  230.6 45.1 %fusion.16 = f32[4,64,96,128]{3,2,1,0:T(8,128)} fusion(f32[4,64,96,128]{3,2,1,0:T(8,128)} %fusion.27, f32[4,64,1,128]{3,2,1,0:T(1,128)} %bitcast.15, f32[6,1,96,128]{3,2,1,0:T(8,128)} %pad.43, f32[6,1,96,128]{3,2,1,0:T(8,128)S(1)} %pad.42, f32[1,64,96,128]{3,2,1,0:T(8,128)} %copy-done.2, f32[1,64,96,128]{3,2,1,0:T(8,128)S(1)} %collective-permute-done.6, ...), kind=kLoop, calls=%fused_computation.35 | loop fusion | flops 119537664 | bytes 44892160 | tf_op jit(solution)/shard_map/add | solution.py:46
  275.6 3.3 fusion.34
  279.0 6.5 %collective-permute-start.13 = (f32[1,64,96,128]{3,2,1,0:T(8,128)S(1)}, f32[1,64,96,128]{3,2,1,0:T(8,128)S(1)}, u32[]{:S(2)}, u32[]{:S(2)}) collective-permute-start(f32[1,64,96,128]{3,2,1,0:T(8,128)S(1)} %get-tuple-element.8), channel_id=1, source_target_pairs={{8,0},{16,8},{24,16},{32,24},{40,32},{48,40},{56,48},{64,56},{72,6... | collective-permute-start | bytes 9437192 | tf_op jit(solution)/shard_map/ppermute | solution.py:18
  286.7 1.7 collective-permute-start.15
  288.4 1.7 fusion.33
  290.2 2.5 collective-permute-start.16
  292.7 63.4 %collective-permute-done.14 = f32[4,1,96,128]{3,2,1,0:T(8,128)S(1)} collective-permute-done((f32[4,1,96,128]{3,2,1,0:T(8,128)S(1)}, f32[4,1,96,128]{3,2,1,0:T(8,128)S(1)}, u32[]{:S(2)}, u32[]{:S(2)}) %collective-permute-start.14) | collective-permute-done | bytes 196640 | tf_op jit(solution)/shard_map/ppermute | solution.py:17
  356.1 1.9 collective-permute-start.17
  358.7 3.9 collective-permute-done.17
  362.6 1.7 copy-done.1
  364.2 45.2 %fusion.5 = f32[4,64,96,128]{3,2,1,0:T(8,128)} fusion(f32[4,64,96,128]{3,2,1,0:T(8,128)} %fusion.16, f32[4,64,1,128]{3,2,1,0:T(1,128)} %bitcast.14, f32[6,1,96,128]{3,2,1,0:T(8,128)} %pad.47, f32[6,1,96,128]{3,2,1,0:T(8,128)S(1)} %pad.46, f32[1,64,96,128]{3,2,1,0:T(8,128)} %copy-done.1, f32[1,64,96,128]{3,2,1,0:T(8,128)S(1)} %collective-permute-done.12, ...), kind=kLoop, calls=%fused_computation.6 | loop fusion | flops 119537664 | bytes 44892160 | tf_op jit(solution)/shard_map/add | solution.py:46
  (39 shorter events, 5.7 us)
Async XLA Ops:
  5.0 80.9 %collective-permute-start = (f32[1,64,96,128]{3,2,1,0:T(8,128)S(1)}, f32[1,64,96,128]{3,2,1,0:T(8,128)S(1)}, u32[]{:S(2)}, u32[]{:S(2)}) collective-permute-start(f32[1,64,96,128]{3,2,1,0:T(8,128)S(1)} %get-tuple-element.22), channel_id=1, source_target_pairs={{0,8},{8,16},{16,24},{24,32},{32,40},{40,48},{48,56},{56,64},{64,7... | collective-permute-start | bytes 9437192 | tf_op jit(solution)/shard_map/ppermute | solution.py:17
  6.4 91.6 %collective-permute-start.1 = (f32[1,64,96,128]{3,2,1,0:T(8,128)}, f32[1,64,96,128]{3,2,1,0:T(8,128)S(1)}, u32[]{:S(2)}, u32[]{:S(2)}) collective-permute-start(f32[1,64,96,128]{3,2,1,0:T(8,128)} %get-tuple-element.21), channel_id=1, source_target_pairs={{8,0},{16,8},{24,16},{32,24},{40,32},{48,40},{56,48},{64,56},{72,6... | collective-permute-start | bytes 9437192 | tf_op jit(solution)/shard_map/ppermute | solution.py:18
  12.8 72.0 %collective-permute-start.2 = (f32[4,1,96,128]{3,2,1,0:T(8,128)S(1)}, f32[4,1,96,128]{3,2,1,0:T(8,128)S(1)}, u32[]{:S(2)}, u32[]{:S(2)}) collective-permute-start(f32[4,1,96,128]{3,2,1,0:T(8,128)S(1)} %get-tuple-element.19), channel_id=1, source_target_pairs={{0,2},{2,4},{4,6},{6,0},{1,3},{3,5},{5,7},{7,1},{8,10},{10,12},{12... | collective-permute-start | bytes 589832 | tf_op jit(solution)/shard_map/ppermute | solution.py:17
  12.9 72.3 %collective-permute-start.3 = (f32[4,1,96,128]{3,2,1,0:T(8,128)S(1)}, f32[4,1,96,128]{3,2,1,0:T(8,128)S(1)}, u32[]{:S(2)}, u32[]{:S(2)}) collective-permute-start(f32[4,1,96,128]{3,2,1,0:T(8,128)S(1)} %get-tuple-element.20), channel_id=1, source_target_pairs={{2,0},{4,2},{6,4},{0,6},{3,1},{5,3},{7,5},{1,7},{10,8},{12,10},{14... | collective-permute-start | bytes 589832 | tf_op jit(solution)/shard_map/ppermute | solution.py:18
  17.1 84.6 %collective-permute-start.5 = (f32[4,64,1,128]{3,1,2,0:T(8,128)}, f32[4,64,1,128]{3,1,2,0:T(8,128)}, u32[]{:S(2)}, u32[]{:S(2)}) collective-permute-start(f32[4,64,1,128]{3,1,2,0:T(8,128)} %bitcast.10), channel_id=1, source_target_pairs={{1,0},{0,1},{3,2},{2,3},{5,4},{4,5},{7,6},{6,7},{9,8},{8,9},{11,10... | collective-permute-start | bytes 393224 | tf_op jit(solution)/shard_map/ppermute | solution.py:18
  84.8 16.9 %collective-permute-start.4 = (f32[4,64,1,128]{3,1,2,0:T(8,128)}, f32[4,64,1,128]{3,1,2,0:T(8,128)}, u32[]{:S(2)}, u32[]{:S(2)}) collective-permute-start(f32[4,64,1,128]{3,1,2,0:T(8,128)} %bitcast.8), channel_id=1, source_target_pairs={{0,1},{1,0},{2,3},{3,2},{4,5},{5,4},{6,7},{7,6},{8,9},{9,8},{10,11... | collective-permute-start | bytes 393224 | tf_op jit(solution)/shard_map/ppermute | solution.py:17
  98.1 1.7 copy-start
  146.2 82.8 %collective-permute-start.6 = (f32[1,64,96,128]{3,2,1,0:T(8,128)S(1)}, f32[1,64,96,128]{3,2,1,0:T(8,128)S(1)}, u32[]{:S(2)}, u32[]{:S(2)}) collective-permute-start(f32[1,64,96,128]{3,2,1,0:T(8,128)S(1)} %get-tuple-element.13), channel_id=1, source_target_pairs={{0,8},{8,16},{16,24},{24,32},{32,40},{40,48},{48,56},{56,64},{64,7... | collective-permute-start | bytes 9437192 | tf_op jit(solution)/shard_map/ppermute | solution.py:17
  146.2 82.7 %collective-permute-start.7 = (f32[1,64,96,128]{3,2,1,0:T(8,128)S(1)}, f32[1,64,96,128]{3,2,1,0:T(8,128)S(1)}, u32[]{:S(2)}, u32[]{:S(2)}) collective-permute-start(f32[1,64,96,128]{3,2,1,0:T(8,128)S(1)} %get-tuple-element.14), channel_id=1, source_target_pairs={{8,0},{16,8},{24,16},{32,24},{40,32},{48,40},{56,48},{64,56},{72,6... | collective-permute-start | bytes 9437192 | tf_op jit(solution)/shard_map/ppermute | solution.py:18
  153.8 68.2 %collective-permute-start.8 = (f32[4,1,96,128]{3,2,1,0:T(8,128)S(1)}, f32[4,1,96,128]{3,2,1,0:T(8,128)S(1)}, u32[]{:S(2)}, u32[]{:S(2)}) collective-permute-start(f32[4,1,96,128]{3,2,1,0:T(8,128)S(1)} %get-tuple-element.15), channel_id=1, source_target_pairs={{0,2},{2,4},{4,6},{6,0},{1,3},{3,5},{5,7},{7,1},{8,10},{10,12},{12... | collective-permute-start | bytes 589832 | tf_op jit(solution)/shard_map/ppermute | solution.py:17
  153.9 70.7 %collective-permute-start.9 = (f32[4,1,96,128]{3,2,1,0:T(8,128)S(1)}, f32[4,1,96,128]{3,2,1,0:T(8,128)S(1)}, u32[]{:S(2)}, u32[]{:S(2)}) collective-permute-start(f32[4,1,96,128]{3,2,1,0:T(8,128)S(1)} %get-tuple-element.16), channel_id=1, source_target_pairs={{2,0},{4,2},{6,4},{0,6},{3,1},{5,3},{7,5},{1,7},{10,8},{12,10},{14... | collective-permute-start | bytes 589832 | tf_op jit(solution)/shard_map/ppermute | solution.py:18
  157.4 67.9 %collective-permute-start.10 = (f32[4,64,1,128]{3,1,2,0:T(8,128)S(1)}, f32[4,64,1,128]{3,1,2,0:T(8,128)S(1)}, u32[]{:S(2)}, u32[]{:S(2)}) collective-permute-start(f32[4,64,1,128]{3,1,2,0:T(8,128)S(1)} %bitcast.19), channel_id=1, source_target_pairs={{0,1},{1,0},{2,3},{3,2},{4,5},{5,4},{6,7},{7,6},{8,9},{9,8},{10,11... | collective-permute-start | bytes 393224 | tf_op jit(solution)/shard_map/ppermute | solution.py:17
  222.0 6.9 %collective-permute-start.11 = (f32[4,64,1,128]{3,1,2,0:T(8,128)S(1)}, f32[4,64,1,128]{3,1,2,0:T(8,128)S(1)}, u32[]{:S(2)}, u32[]{:S(2)}) collective-permute-start(f32[4,64,1,128]{3,1,2,0:T(8,128)S(1)} %bitcast.17), channel_id=1, source_target_pairs={{1,0},{0,1},{3,2},{2,3},{5,4},{4,5},{7,6},{6,7},{9,8},{8,9},{11,10... | collective-permute-start | bytes 393224 | tf_op jit(solution)/shard_map/ppermute | solution.py:18
  225.3 5.3 %copy-start.4 = (f32[4,64,1,128]{3,1,2,0:T(8,128)}, f32[4,64,1,128]{3,1,2,0:T(8,128)S(1)}, u32[]{:S(2)}) copy-start(f32[4,64,1,128]{3,1,2,0:T(8,128)S(1)} %collective-permute-done.10) | copy-start | bytes 393220
  228.9 1.7 copy-start.6
  228.9 1.7 copy-start.2
  278.9 83.6 %collective-permute-start.12 = (f32[1,64,96,128]{3,2,1,0:T(8,128)S(1)}, f32[1,64,96,128]{3,2,1,0:T(8,128)S(1)}, u32[]{:S(2)}, u32[]{:S(2)}) collective-permute-start(f32[1,64,96,128]{3,2,1,0:T(8,128)S(1)} %get-tuple-element.7), channel_id=1, source_target_pairs={{0,8},{8,16},{16,24},{24,32},{32,40},{40,48},{48,56},{56,64},{64,7... | collective-permute-start | bytes 9437192 | tf_op jit(solution)/shard_map/ppermute | solution.py:17
  279.0 83.5 %collective-permute-start.13 = (f32[1,64,96,128]{3,2,1,0:T(8,128)S(1)}, f32[1,64,96,128]{3,2,1,0:T(8,128)S(1)}, u32[]{:S(2)}, u32[]{:S(2)}) collective-permute-start(f32[1,64,96,128]{3,2,1,0:T(8,128)S(1)} %get-tuple-element.8), channel_id=1, source_target_pairs={{8,0},{16,8},{24,16},{32,24},{40,32},{48,40},{56,48},{64,56},{72,6... | collective-permute-start | bytes 9437192 | tf_op jit(solution)/shard_map/ppermute | solution.py:18
  286.6 69.5 %collective-permute-start.14 = (f32[4,1,96,128]{3,2,1,0:T(8,128)S(1)}, f32[4,1,96,128]{3,2,1,0:T(8,128)S(1)}, u32[]{:S(2)}, u32[]{:S(2)}) collective-permute-start(f32[4,1,96,128]{3,2,1,0:T(8,128)S(1)} %get-tuple-element.9), channel_id=1, source_target_pairs={{0,2},{2,4},{4,6},{6,0},{1,3},{3,5},{5,7},{7,1},{8,10},{10,12},{12... | collective-permute-start | bytes 589832 | tf_op jit(solution)/shard_map/ppermute | solution.py:17
  286.7 71.3 %collective-permute-start.15 = (f32[4,1,96,128]{3,2,1,0:T(8,128)S(1)}, f32[4,1,96,128]{3,2,1,0:T(8,128)S(1)}, u32[]{:S(2)}, u32[]{:S(2)}) collective-permute-start(f32[4,1,96,128]{3,2,1,0:T(8,128)S(1)} %get-tuple-element.10), channel_id=1, source_target_pairs={{2,0},{4,2},{6,4},{0,6},{3,1},{5,3},{7,5},{1,7},{10,8},{12,10},{14... | collective-permute-start | bytes 589832 | tf_op jit(solution)/shard_map/ppermute | solution.py:18
  290.2 68.5 %collective-permute-start.16 = (f32[4,64,1,128]{3,1,2,0:T(8,128)S(1)}, f32[4,64,1,128]{3,1,2,0:T(8,128)S(1)}, u32[]{:S(2)}, u32[]{:S(2)}) collective-permute-start(f32[4,64,1,128]{3,1,2,0:T(8,128)S(1)} %bitcast.18), channel_id=1, source_target_pairs={{0,1},{1,0},{2,3},{3,2},{4,5},{5,4},{6,7},{7,6},{8,9},{9,8},{10,11... | collective-permute-start | bytes 393224 | tf_op jit(solution)/shard_map/ppermute | solution.py:17
  356.1 6.5 %collective-permute-start.17 = (f32[4,64,1,128]{3,1,2,0:T(8,128)S(1)}, f32[4,64,1,128]{3,1,2,0:T(8,128)S(1)}, u32[]{:S(2)}, u32[]{:S(2)}) collective-permute-start(f32[4,64,1,128]{3,1,2,0:T(8,128)S(1)} %bitcast.16), channel_id=1, source_target_pairs={{1,0},{0,1},{3,2},{2,3},{5,4},{4,5},{7,6},{6,7},{9,8},{8,9},{11,10... | collective-permute-start | bytes 393224 | tf_op jit(solution)/shard_map/ppermute | solution.py:18
  358.7 5.5 %copy-start.3 = (f32[4,64,1,128]{3,1,2,0:T(8,128)}, f32[4,64,1,128]{3,1,2,0:T(8,128)S(1)}, u32[]{:S(2)}) copy-start(f32[4,64,1,128]{3,1,2,0:T(8,128)S(1)} %collective-permute-done.16) | copy-start | bytes 393220
  362.5 1.7 copy-start.5
  362.6 1.7 copy-start.1
where the time goes:
time: 411 us; the launch traced here: 410 us
  waiting for transfers between devices  199 us (48%)
  other arithmetic  131 us (32%)
  local copies, waits for them, and re-layouts  41.9 us (10%)
  starting transfers between devices  36.6 us (9%)
    ppermute x9, waiting for transfers between devices, with_halo(): lax.ppermute(last, axis, up)  192 us
    add x3, other arithmetic, march_step(): return middle + 0.1 * spread + 0.2 * middle * (1.0 - middle * crowding)  131 us
    ppermute x9, starting transfers between devices, with_halo(): lax.ppermute(first, axis, [(b, a) for a, b in up])  28.6 us
    unnamed x16, local copies, waits for them, and re-layouts  17.2 us
    slice x8, local copies, waits for them, and re-layouts, with_halo(): last = lax.slice_in_dim(x, length - width, length, axis=dim)  15.7 us
  transfers between devices with their start and end apart: 18, of which 5 were waited for; matrix products, arithmetic and copies ran while one was open for 6% of the time, Pallas kernels for 0%

commit v1 on v0

v1 whole, which is shorter than its diff:
```python
import functools

import jax
import jax.numpy as jnp
from jax import lax
from jax.experimental import pallas as pl
from jax.experimental.pallas import tpu as pltpu
from jax.sharding import PartitionSpec as P

STEPS = 3
ROWS = 4
AHEAD = 3
GROUPS = 4
LOW, HIGH = 0, 1


def kernel(
    field, crowding, out,
    even, odd, crowd, lat_halo, lev_face, lev_halo,
    load_sem, out_sem, lat_send, lat_recv, lon_send, lon_recv, lev_send, lev_recv,
):
    depth, width, tall, _ = field.shape
    chunks = width // ROWS
    each = chunks // GROUPS
    bufs = (even, odd)

    def beside(axis, step):
        size = lax.axis_size(axis)
        return {axis: lax.rem(lax.axis_index(axis) + step + size, size)}

    lat_at = (beside("lat", -1), beside("lat", 1))
    lon_at = (beside("lon", -1), beside("lon", 1))
    lev_at = (beside("lev", -1), beside("lev", 1))

    def chunk_at(n):
        return jnp.where(n == 0, 0, jnp.where(n == 1, chunks - 1, n - 1))

    load_field = pltpu.make_async_copy(field, even.at[:, pl.ds(1, width)], load_sem.at[0])
    load_crowd = pltpu.make_async_copy(crowding, crowd, load_sem.at[1])

    def lat_copy(t, side, n):
        plane = depth - 1 if side == LOW else 0
        rows = chunk_at(n) * ROWS
        if t == 0:
            src = field.at[plane, pl.ds(rows, ROWS)]
        else:
            src = bufs[t % 2].at[plane, pl.ds(rows + 1, ROWS)]
        return pltpu.make_async_remote_copy(
            src_ref=src,
            dst_ref=lat_halo.at[t % 2, side, pl.ds(rows, ROWS)],
            send_sem=lat_send.at[side, n],
            recv_sem=lat_recv.at[t % 2, side, n],
            device_id=lat_at[1 - side],
            device_id_type=pl.DeviceIdType.MESH,
        )

    def lon_copy(t, side):
        row = width - 1 if side == LOW else 0
        src = field.at[:, row] if t == 0 else bufs[t % 2].at[:, row + 1]
        return pltpu.make_async_remote_copy(
            src_ref=src,
            dst_ref=bufs[t % 2].at[:, 0 if side == LOW else width + 1],
            send_sem=lon_send.at[t, side],
            recv_sem=lon_recv.at[t, side],
            device_id=lon_at[1 - side],
            device_id_type=pl.DeviceIdType.MESH,
        )

    def lev_copy(t, side, group):
        rows = pl.ds(group * (each * ROWS), each * ROWS)
        return pltpu.make_async_remote_copy(
            src_ref=lev_face.at[t, side, rows],
            dst_ref=lev_halo.at[t, side, rows],
            send_sem=lev_send.at[t, side, group],
            recv_sem=lev_recv.at[t, side, group],
            device_id=lev_at[1 - side],
            device_id_type=pl.DeviceIdType.MESH,
        )

    def out_copy(n):
        rows = chunk_at(n) * ROWS
        return pltpu.make_async_copy(
            odd.at[:, pl.ds(rows + 1, ROWS)], out.at[:, pl.ds(rows, ROWS)], out_sem.at[n]
        )

    def both(copy, *where):
        return [copy(*(where[:1] + (side,) + where[1:])) for side in (LOW, HIGH)]

    load_field.start()
    load_crowd.start()
    barrier = pltpu.get_barrier_semaphore()
    partners = (*lat_at, *lon_at, lev_at[0])
    for partner in partners:
        pl.semaphore_signal(barrier, inc=1, device_id=partner, device_id_type=pl.DeviceIdType.MESH)
    pl.semaphore_wait(barrier, len(partners))

    for n in range(AHEAD):
        for copy in both(lat_copy, 0, n):
            copy.start()
    for copy in both(lon_copy, 0):
        copy.start()
    load_field.wait()

    def pack(position, carry):
        n = position // ROWS
        row = chunk_at(n) * ROWS + position % ROWS + 1
        for plane in range(depth):
            lev_face[0, LOW, position, pl.ds(plane, 1)] = even[plane, row, pl.ds(tall - 1, 1)]
            lev_face[0, HIGH, position, pl.ds(plane, 1)] = even[plane, row, pl.ds(0, 1)]
        return carry

    lax.fori_loop(0, width, pack, 0)
    for group in range(GROUPS):
        for copy in both(lev_copy, 0, group):
            copy.start()
    load_crowd.wait()

    edge = lax.broadcasted_iota(jnp.int32, (8, 128), 0)

    def new_row(s, n, r):
        src, dst = bufs[s % 2], bufs[(s + 1) % 2]
        at = chunk_at(n) * ROWS + r
        row, position = at + 1, n * ROWS + r
        for plane in range(depth):
            for start, stop in ((0, 8), (8, 32), (32, 64), (64, tall - 8), (tall - 8, tall)):
                span = pl.ds(start, stop - start)
                middle = src[plane, row, span]
                if start == 0:
                    halo = lev_halo[s, LOW, position, pl.ds(plane, 1)]
                    lower = jnp.where(edge == 0, halo, pltpu.roll(middle, 1, 0))
                else:
                    lower = src[plane, row, pl.ds(start - 1, stop - start)]
                if stop == tall:
                    halo = lev_halo[s, HIGH, position, pl.ds(plane, 1)]
                    upper = jnp.where(edge == 7, halo, pltpu.roll(middle, 7, 0))
                else:
                    upper = src[plane, row, pl.ds(start + 1, stop - start)]
                around = lower + upper + src[plane, row - 1, span] + src[plane, row + 1, span]
                if plane == 0:
                    around += lat_halo[s % 2, LOW, at, span]
                else:
                    around += src[plane - 1, row, span]
                if plane == depth - 1:
                    around += lat_halo[s % 2, HIGH, at, span]
                else:
                    around += src[plane + 1, row, span]
                growth = 0.6 - 0.2 * (middle * crowd[plane, at, span])
                new = 0.1 * around + middle * growth
                dst[plane, row, span] = new
                if s < STEPS - 1:
                    if start == 0:
                        lev_face[s + 1, HIGH, position, pl.ds(plane, 1)] = new[0:1]
                    if stop == tall:
                        lev_face[s + 1, LOW, position, pl.ds(plane, 1)] = new[7:8]

    for s in range(STEPS):

        def chunk(n, carry, s=s):
            for copy in both(lat_copy, s, n):
                copy.wait_recv()

            @pl.when(n + AHEAD < chunks)
            def _():
                if s > 0:
                    for copy in both(lat_copy, s - 1, n + AHEAD):
                        copy.wait_send()
                for copy in both(lat_copy, s, n + AHEAD):
                    copy.start()

            if s < STEPS - 1:

                @pl.when(n + AHEAD >= chunks)
                def _():
                    for copy in both(lat_copy, s, n + AHEAD - chunks):
                        copy.wait_send()
                    for copy in both(lat_copy, s + 1, n + AHEAD - chunks):
                        copy.start()

            @pl.when(n == 0)
            def _():
                if s > 0:
                    for copy in both(lev_copy, s, GROUPS - 1):
                        copy.start()
                    for copy in both(lon_copy, s - 1):
                        copy.wait_send()
                for copy in both(lon_copy, s):
                    copy.wait_recv()

            if s < STEPS - 1:

                @pl.when(n == 2)
                def _():
                    for copy in both(lon_copy, s + 1):
                        copy.start()

            @pl.when(n % each == 0)
            def _():
                for copy in both(lev_copy, s, n // each):
                    copy.wait_recv()
                if s < STEPS - 1:

                    @pl.when(n > 0)
                    def _():
                        for copy in both(lev_copy, s + 1, n // each - 1):
                            copy.start()

            if s == STEPS - 1:

                @pl.when(n > 0)
                def _():
                    out_copy(n - 1).start()

            def row(r, inner):
                new_row(s, n, r)
                return inner

            return lax.fori_loop(0, ROWS, row, carry)

        lax.fori_loop(0, chunks, chunk, 0)

    out_copy(chunks - 1).start()

    def drain(n, carry):
        for copy in both(lat_copy, STEPS - 1, n):
            copy.wait_send()
        out_copy(n).wait()
        return carry

    for copy in both(lon_copy, STEPS - 1):
        copy.wait_send()
    for t in range(STEPS):
        for group in range(GROUPS):
            for copy in both(lev_copy, t, group):
                copy.wait_send()
    lax.fori_loop(0, chunks, drain, 0)


def local(field, crowding):
    depth, width, tall, lanes = field.shape
    chunks = width // ROWS
    padded = (depth, width + 2, tall, lanes)
    faces = (STEPS, 2, width, depth, lanes)
    dma = pltpu.SemaphoreType.DMA
    return pl.pallas_call(
        kernel,
        out_shape=jax.ShapeDtypeStruct(field.shape, field.dtype),
        in_specs=[pl.BlockSpec(memory_space=pl.ANY)] * 2,
        out_specs=pl.BlockSpec(memory_space=pl.ANY),
        scratch_shapes=[
            pltpu.VMEM(padded, jnp.float32),
            pltpu.VMEM(padded, jnp.float32),
            pltpu.VMEM(field.shape, jnp.float32),
            pltpu.VMEM((2, 2, width, tall, lanes), jnp.float32),
            pltpu.VMEM(faces, jnp.float32),
            pltpu.VMEM(faces, jnp.float32),
            dma((2,)),
            dma((chunks,)),
            dma((2, chunks)),
            dma((2, 2, chunks)),
            dma((STEPS, 2)),
            dma((STEPS, 2)),
            dma((STEPS, 2, GROUPS)),
            dma((STEPS, 2, GROUPS)),
        ],
        compiler_params=pltpu.CompilerParams(
            collective_id=0, has_side_effects=True, vmem_limit_bytes=60 * 1024 * 1024
        ),
        name="march",
    )(field, crowding)


def solution(mesh):
    spec = P("lat", "lon", "lev", None)
    return jax.shard_map(
        local, mesh=mesh, in_specs=(spec, spec), out_specs=spec, check_vma=False
    )
```

time: 411 us -> 429 us (1.044)
  the two profiles are of different devices: /device:TPU:16 before, /device:TPU:38 now
where the time goes in v1:
time: 429 us
  Pallas kernels  418 us (97%)
  local copies, waits for them, and re-layouts  10.6 us (2%)
    pallas_call x1, Pallas kernels, local(): pl.pallas_call(kernel, out_shape=jax.ShapeDtypeStruct(field.shape, field....  418 us
    unnamed x1, local copies, waits for them, and re-layouts  10.6 us

profile of v1, /device:TPU:38, one launch (start us, length us, event | category | flops | bytes accessed | tf_op | source)
XLA Modules:
  0.0 428.8 jit_solution(9517221595394122247)
XLA Ops:
  0.0 418.2 %march.1 = f32[4,64,96,128]{3,2,1,0:T(8,128)} custom-call(f32[4,64,96,128]{3,2,1,0:T(8,128)} %field.1, f32[4,64,96,128]{3,2,1,0:T(8,128)} %crowding.1), custom_call_target="tpu_custom_call" | custom-call | tf_op jit(solution)/shard_map/march/pallas_call | solution.py:244
  418.2 10.6 %copy.4 = f32[4,64,96,128]{3,2,1,0:T(8,128)} copy(f32[4,64,96,128]{3,2,1,0:T(8,128)} %march.1) | data formatting | bytes 25165824

commit v2 on v1

--- a/solution.py
+++ b/solution.py
@@ -8,16 +8,20 @@
 from jax.sharding import PartitionSpec as P
 
 STEPS = 3
-ROWS = 4
-AHEAD = 3
+ROWS = 2
+AHEAD = 16
+LEADS = (8, 6)
+SETTLE = 6
+DIRECT = 12
 GROUPS = 4
 LOW, HIGH = 0, 1
 
 
 def kernel(
     field, crowding, out,
-    even, odd, crowd, lat_halo, lev_face, lev_halo,
+    even, odd, crowd, lat_halo, lev_face, lev_halo, relay,
     load_sem, out_sem, lat_send, lat_recv, lon_send, lon_recv, lev_send, lev_recv,
+    relay_send, relay_recv,
 ):
     depth, width, tall, _ = field.shape
     chunks = width // ROWS
@@ -31,6 +35,16 @@
     lat_at = (beside("lat", -1), beside("lat", 1))
     lon_at = (beside("lon", -1), beside("lon", 1))
     lev_at = (beside("lev", -1), beside("lev", 1))
+
+    lat = lax.axis_index("lat")
+    x, y = lat % 4, (lat // 4) % 2
+    first, last = x == 0, x == 3
+    edge = first | last
+    corner = (first & (y == 0)) | (last & (y == 1))
+    mine = jnp.where(first, LOW, HIGH)
+    across = {"lat": jnp.where(first, lat + 3, jnp.where(last, lat - 3, lat))}
+    turned = {"lat": jnp.where(y == 0, lat + 4, lat - 4)}
+    lifted = {"lat": lax.rem(lat + 8, 16)}
 
     def chunk_at(n):
         return jnp.where(n == 0, 0, jnp.where(n == 1, chunks - 1, n - 1))
@@ -54,6 +68,91 @@
             device_id_type=pl.DeviceIdType.MESH,
         )
 
+    def lat_start(t, side, n):
+        plain = lat_copy(t, side, n)
+        leaves = last if side == LOW else first
+        if t == STEPS - 1:
+            leaves = leaves & (n < DIRECT)
+
+        @pl.when(leaves)
+        def _():
+            pltpu.make_async_remote_copy(
+                src_ref=plain.src_ref,
+                dst_ref=relay.at[0, pl.ds(chunk_at(n) * ROWS, ROWS)],
+                send_sem=lat_send.at[side, n],
+                recv_sem=relay_recv.at[0, n],
+                device_id=across,
+                device_id_type=pl.DeviceIdType.MESH,
+            ).start()
+
+        @pl.when(jnp.logical_not(leaves))
+        def _():
+            plain.start()
+
+    def relay_copy(t, stage, n, arrives):
+        rows = pl.ds(chunk_at(n) * ROWS, ROWS)
+        return pltpu.make_async_remote_copy(
+            src_ref=relay.at[stage, rows],
+            dst_ref=lat_halo.at[t % 2, mine, rows] if arrives else relay.at[1, rows],
+            send_sem=relay_send.at[stage, n],
+            recv_sem=lat_recv.at[t % 2, mine, n] if arrives else relay_recv.at[1, n],
+            device_id=lifted if stage else turned,
+            device_id_type=pl.DeviceIdType.MESH,
+        )
+
+    def relay_landed(stage, n):
+        rows = pl.ds(chunk_at(n) * ROWS, ROWS)
+        pltpu.make_async_remote_copy(
+            src_ref=relay.at[stage, rows],
+            dst_ref=relay.at[stage, rows],
+            send_sem=relay_send.at[stage, n],
+            recv_sem=relay_recv.at[stage, n],
+            device_id=lifted,
+            device_id_type=pl.DeviceIdType.MESH,
+        ).wait_recv()
+
+    def send_on(t, stage, n):
+        relay_landed(stage, n)
+        if stage == 1:
+            relay_copy(t, stage, n, True).start()
+            return
+
+        @pl.when(corner)
+        def _():
+            relay_copy(t, stage, n, True).start()
+
+        @pl.when(jnp.logical_not(corner))
+        def _():
+            relay_copy(t, stage, n, False).start()
+
+    def relays(s, n):
+        for stage, (lead, there) in enumerate(zip(LEADS, (edge, corner))):
+            ahead = n + lead
+            here = there & (ahead < (DIRECT if s == STEPS - 1 else chunks))
+
+            @pl.when(here)
+            def _():
+                send_on(s, stage, ahead)
+
+            if s < STEPS - 1:
+                end = DIRECT if s + 1 == STEPS - 1 else chunks
+
+                @pl.when(there & (ahead >= chunks) & (ahead - chunks < end))
+                def _():
+                    send_on(s + 1, stage, ahead - chunks)
+
+            left = n - SETTLE
+
+            @pl.when(there & (left >= 0) & (left < (DIRECT if s == STEPS - 1 else chunks)))
+            def _():
+                relay_copy(s, stage, left, True).wait_send()
+
+            if s > 0:
+
+                @pl.when(there & (left < 0))
+                def _():
+                    relay_copy(s - 1, stage, left + chunks, True).wait_send()
+
     def lon_copy(t, side):
         row = width - 1 if side == LOW else 0
         src = field.at[:, row] if t == 0 else bufs[t % 2].at[:, row + 1]
@@ -89,16 +188,30 @@
     load_field.start()
     load_crowd.start()
     barrier = pltpu.get_barrier_semaphore()
-    partners = (*lat_at, *lon_at, lev_at[0])
-    for partner in partners:
-        pl.semaphore_signal(barrier, inc=1, device_id=partner, device_id_type=pl.DeviceIdType.MESH)
-    pl.semaphore_wait(barrier, len(partners))
-
-    for n in range(AHEAD):
-        for copy in both(lat_copy, 0, n):
-            copy.start()
+
+    def greet(partners):
+        for partner in partners:
+            pl.semaphore_signal(
+                barrier, inc=1, device_id=partner, device_id_type=pl.DeviceIdType.MESH
+            )
+
+    greet((*lat_at, *lon_at, lev_at[0]))
+
+    @pl.when(edge)
+    def _():
+        greet((across, turned, lifted))
+
+    pl.semaphore_wait(barrier, jnp.where(edge, 8, 5))
+
     for copy in both(lon_copy, 0):
         copy.start()
+
+    def launch(n, carry):
+        for side in (LOW, HIGH):
+            lat_start(0, side, n)
+        return carry
+
+    lax.fori_loop(0, AHEAD, launch, 0)
     load_field.wait()
 
     def pack(position, carry):
@@ -115,7 +228,17 @@
             copy.start()
     load_crowd.wait()
 
-    edge = lax.broadcasted_iota(jnp.int32, (8, 128), 0)
+    for stage, (lead, there) in enumerate(zip(LEADS, (edge, corner))):
+
+        @pl.when(there)
+        def _(stage=stage, lead=lead):
+            def begin(n, carry):
+                send_on(0, stage, n)
+                return carry
+
+            lax.fori_loop(0, lead, begin, 0)
+
+    place = lax.broadcasted_iota(jnp.int32, (8, 128), 0)
 
     def new_row(s, n, r):
         src, dst = bufs[s % 2], bufs[(s + 1) % 2]
@@ -127,12 +250,12 @@
                 middle = src[plane, row, span]
                 if start == 0:
                     halo = lev_halo[s, LOW, position, pl.ds(plane, 1)]
-                    lower = jnp.where(edge == 0, halo, pltpu.roll(middle, 1, 0))
+                    lower = jnp.where(place == 0, halo, pltpu.roll(middle, 1, 0))
                 else:
                     lower = src[plane, row, pl.ds(start - 1, stop - start)]
                 if stop == tall:
                     halo = lev_halo[s, HIGH, position, pl.ds(plane, 1)]
-                    upper = jnp.where(edge == 7, halo, pltpu.roll(middle, 7, 0))
+                    upper = jnp.where(place == 7, halo, pltpu.roll(middle, 7, 0))
                 else:
                     upper = src[plane, row, pl.ds(start + 1, stop - start)]
                 around = lower + upper + src[plane, row - 1, span] + src[plane, row + 1, span]
@@ -156,6 +279,7 @@
     for s in range(STEPS):
 
         def chunk(n, carry, s=s):
+            relays(s, n)
             for copy in both(lat_copy, s, n):
                 copy.wait_recv()
 
@@ -164,8 +288,8 @@
                 if s > 0:
                     for copy in both(lat_copy, s - 1, n + AHEAD):
                         copy.wait_send()
-                for copy in both(lat_copy, s, n + AHEAD):
-                    copy.start()
+                for side in (LOW, HIGH):
+                    lat_start(s, side, n + AHEAD)
 
             if s < STEPS - 1:
 
@@ -173,8 +297,8 @@
                 def _():
                     for copy in both(lat_copy, s, n + AHEAD - chunks):
                         copy.wait_send()
-                    for copy in both(lat_copy, s + 1, n + AHEAD - chunks):
-                        copy.start()
+                    for side in (LOW, HIGH):
+                        lat_start(s + 1, side, n + AHEAD - chunks)
 
             @pl.when(n == 0)
             def _():
@@ -253,6 +377,7 @@
             pltpu.VMEM((2, 2, width, tall, lanes), jnp.float32),
             pltpu.VMEM(faces, jnp.float32),
             pltpu.VMEM(faces, jnp.float32),
+            pltpu.VMEM((2, width, tall, lanes), jnp.float32),
             dma((2,)),
             dma((chunks,)),
             dma((2, chunks)),
@@ -261,6 +386,8 @@
             dma((STEPS, 2)),
             dma((STEPS, 2, GROUPS)),
             dma((STEPS, 2, GROUPS)),
+            dma((2, chunks)),
+            dma((2, chunks)),
         ],
         compiler_params=pltpu.CompilerParams(
             collective_id=0, has_side_effects=True, vmem_limit_bytes=60 * 1024 * 1024

time: 429 us -> 273 us (0.64)
  the two profiles are of different devices: /device:TPU:38 before, /device:TPU:16 now
where the time goes in v2:
time: 273 us; the launch traced here: 272 us
  Pallas kernels  262 us (96%)
  local copies, waits for them, and re-layouts  10.6 us (4%)
    pallas_call x1, Pallas kernels, local(): pl.pallas_call(kernel, out_shape=jax.ShapeDtypeStruct(field.shape, field....  262 us
    unnamed x1, local copies, waits for them, and re-layouts  10.6 us

profile of v2, /device:TPU:16, one launch (start us, length us, event | category | flops | bytes accessed | tf_op | source)
XLA Modules:
  0.0 272.4 jit_solution(15444263524967135432)
XLA Ops:
  0.0 261.8 %march.1 = f32[4,64,96,128]{3,2,1,0:T(8,128)} custom-call(f32[4,64,96,128]{3,2,1,0:T(8,128)} %field.1, f32[4,64,96,128]{3,2,1,0:T(8,128)} %crowding.1), custom_call_target="tpu_custom_call" | custom-call | tf_op jit(solution)/shard_map/march/pallas_call | solution.py:368
  261.8 10.6 %copy.4 = f32[4,64,96,128]{3,2,1,0:T(8,128)} copy(f32[4,64,96,128]{3,2,1,0:T(8,128)} %march.1) | data formatting | bytes 25165824

commit v3 on v2

--- a/solution.py
+++ b/solution.py
@@ -9,18 +9,18 @@
 
 STEPS = 3
 ROWS = 2
-AHEAD = 16
-LEADS = (8, 6)
+AHEAD = 12
+LEADS = (4, 2)
 SETTLE = 6
-DIRECT = 12
+DIRECT = 32
 GROUPS = 4
 LOW, HIGH = 0, 1
 
 
 def kernel(
-    field, crowding, out,
-    even, odd, crowd, lat_halo, lev_face, lev_halo, relay,
-    load_sem, out_sem, lat_send, lat_recv, lon_send, lon_recv, lev_send, lev_recv,
+    field, crowding, crowd,
+    even, odd, lat_halo, lev_face, lev_halo, relay,
+    load_sem, lat_send, lat_recv, lon_send, lon_recv, lev_send, lev_recv,
     relay_send, relay_recv,
 ):
     depth, width, tall, _ = field.shape
@@ -176,12 +176,6 @@
             device_id_type=pl.DeviceIdType.MESH,
         )
 
-    def out_copy(n):
-        rows = chunk_at(n) * ROWS
-        return pltpu.make_async_copy(
-            odd.at[:, pl.ds(rows + 1, ROWS)], out.at[:, pl.ds(rows, ROWS)], out_sem.at[n]
-        )
-
     def both(copy, *where):
         return [copy(*(where[:1] + (side,) + where[1:])) for side in (LOW, HIGH)]
 
@@ -269,7 +263,10 @@
                     around += src[plane + 1, row, span]
                 growth = 0.6 - 0.2 * (middle * crowd[plane, at, span])
                 new = 0.1 * around + middle * growth
-                dst[plane, row, span] = new
+                if s == STEPS - 1:
+                    crowd[plane, at, span] = new
+                else:
+                    dst[plane, row, span] = new
                 if s < STEPS - 1:
                     if start == 0:
                         lev_face[s + 1, HIGH, position, pl.ds(plane, 1)] = new[0:1]
@@ -328,12 +325,6 @@
                         for copy in both(lev_copy, s + 1, n // each - 1):
                             copy.start()
 
-            if s == STEPS - 1:
-
-                @pl.when(n > 0)
-                def _():
-                    out_copy(n - 1).start()
-
             def row(r, inner):
                 new_row(s, n, r)
                 return inner
@@ -342,12 +333,9 @@
 
         lax.fori_loop(0, chunks, chunk, 0)
 
-    out_copy(chunks - 1).start()
-
     def drain(n, carry):
         for copy in both(lat_copy, STEPS - 1, n):
             copy.wait_send()
-        out_copy(n).wait()
         return carry
 
     for copy in both(lon_copy, STEPS - 1):
@@ -357,6 +345,16 @@
             for copy in both(lev_copy, t, group):
                 copy.wait_send()
     lax.fori_loop(0, chunks, drain, 0)
+
+    for stage, there in enumerate((edge, corner)):
+
+        @pl.when(there)
+        def _(stage=stage):
+            def settle(n, carry):
+                relay_copy(STEPS - 1, stage, n, True).wait_send()
+                return carry
+
+            lax.fori_loop(chunks - SETTLE, DIRECT, settle, 0)
 
 
 def local(field, crowding):
@@ -367,19 +365,17 @@
     dma = pltpu.SemaphoreType.DMA
     return pl.pallas_call(
         kernel,
-        out_shape=jax.ShapeDtypeStruct(field.shape, field.dtype),
+        out_shape=pltpu.VMEM(field.shape, field.dtype),
         in_specs=[pl.BlockSpec(memory_space=pl.ANY)] * 2,
-        out_specs=pl.BlockSpec(memory_space=pl.ANY),
+        out_specs=pl.BlockSpec(memory_space=pltpu.VMEM),
         scratch_shapes=[
             pltpu.VMEM(padded, jnp.float32),
             pltpu.VMEM(padded, jnp.float32),
-            pltpu.VMEM(field.shape, jnp.float32),
             pltpu.VMEM((2, 2, width, tall, lanes), jnp.float32),
             pltpu.VMEM(faces, jnp.float32),
             pltpu.VMEM(faces, jnp.float32),
             pltpu.VMEM((2, width, tall, lanes), jnp.float32),
             dma((2,)),
-            dma((chunks,)),
             dma((2, chunks)),
             dma((2, 2, chunks)),
             dma((STEPS, 2)),
@@ -390,7 +386,7 @@
             dma((2, chunks)),
         ],
         compiler_params=pltpu.CompilerParams(
-            collective_id=0, has_side_effects=True, vmem_limit_bytes=60 * 1024 * 1024
+            collective_id=0, has_side_effects=True, vmem_limit_bytes=46 * 1024 * 1024
         ),
         name="march",
     )(field, crowding)

time: 273 us -> 243 us (0.89)
  Pallas kernels: 262 us -> 238 us
  local copies, waits for them, and re-layouts: 10.6 us -> 4.78 us
    pallas_call x1, Pallas kernels: 262 us -> 238 us  [local(): pl.pallas_call(kernel, out_shape=pltpu.VMEM(field.shape, field.dtype), in...]
    unnamed x1, local copies, waits for them, and re-layouts: 10.6 us -> 4.78 us
where the time goes in v3:
time: 243 us; the launch traced here: 242 us
  Pallas kernels  238 us (98%)
  local copies, waits for them, and re-layouts  4.78 us (2%)
    pallas_call x1, Pallas kernels, local(): pl.pallas_call(kernel, out_shape=pltpu.VMEM(field.shape, field.dtype), in...  238 us

profile of v3, /device:TPU:16, one launch (start us, length us, event | category | flops | bytes accessed | tf_op | source)
XLA Modules:
  0.0 242.4 jit_solution(477261571318548448)
XLA Ops:
  0.0 237.6 %march.1 = f32[4,64,96,128]{3,2,1,0:T(8,128)S(1)} custom-call(f32[4,64,96,128]{3,2,1,0:T(8,128)} %field.1, f32[4,64,96,128]{3,2,1,0:T(8,128)} %crowding.1), custom_call_target="tpu_custom_call" | custom-call | tf_op jit(solution)/shard_map/march/pallas_call | solution.py:366
  237.6 4.8 %copy.4 = f32[4,64,96,128]{3,2,1,0:T(8,128)} copy(f32[4,64,96,128]{3,2,1,0:T(8,128)S(1)} %march.1) | data formatting | bytes 25165824

commit v4 on v3

--- a/solution.py
+++ b/solution.py
@@ -9,19 +9,20 @@
 
 STEPS = 3
 ROWS = 2
-AHEAD = 12
+AHEAD = 10
 LEADS = (4, 2)
 SETTLE = 6
 DIRECT = 32
+PASS = 10
 GROUPS = 4
 LOW, HIGH = 0, 1
 
 
 def kernel(
     field, crowding, crowd,
-    even, odd, lat_halo, lev_face, lev_halo, relay,
+    even, odd, lat_halo, lev_face, lev_halo, relay, lev_pass,
     load_sem, lat_send, lat_recv, lon_send, lon_recv, lev_send, lev_recv,
-    relay_send, relay_recv,
+    relay_send, relay_recv, pass_send, pass_recv,
 ):
     depth, width, tall, _ = field.shape
     chunks = width // ROWS
@@ -45,6 +46,10 @@
     across = {"lat": jnp.where(first, lat + 3, jnp.where(last, lat - 3, lat))}
     turned = {"lat": jnp.where(y == 0, lat + 4, lat - 4)}
     lifted = {"lat": lax.rem(lat + 8, 16)}
+
+    inside = lat + jnp.where(x % 2 == 0, 1, -1)
+    aslant = {"lat": inside, **beside("lev", 1)}
+    inward = {"lat": inside}
 
     def chunk_at(n):
         return jnp.where(n == 0, 0, jnp.where(n == 1, chunks - 1, n - 1))
@@ -176,6 +181,49 @@
             device_id_type=pl.DeviceIdType.MESH,
         )
 
+    def lev_start(t, group):
+        plain = lev_copy(t, HIGH, group)
+        lev_copy(t, LOW, group).start()
+        if t == 0:
+            plain.start()
+            return
+
+        @pl.when(edge)
+        def _():
+            pltpu.make_async_remote_copy(
+                src_ref=plain.src_ref,
+                dst_ref=lev_pass.at[t, pl.ds(group * (each * ROWS), each * ROWS)],
+                send_sem=lev_send.at[t, HIGH, group],
+                recv_sem=pass_recv.at[t, group],
+                device_id=aslant,
+                device_id_type=pl.DeviceIdType.MESH,
+            ).start()
+
+        @pl.when(jnp.logical_not(edge))
+        def _():
+            plain.start()
+
+    def pass_copy(t, group, landing=False):
+        rows = pl.ds(group * (each * ROWS), each * ROWS)
+        return pltpu.make_async_remote_copy(
+            src_ref=lev_pass.at[t, rows],
+            dst_ref=lev_pass.at[t, rows] if landing else lev_halo.at[t, HIGH, rows],
+            send_sem=pass_send.at[t, group],
+            recv_sem=pass_recv.at[t, group] if landing else lev_recv.at[t, HIGH, group],
+            device_id=inward,
+            device_id_type=pl.DeviceIdType.MESH,
+        )
+
+    def pass_on(s, n):
+        for t, since in ((s + 1, n - each - PASS), (s, n + chunks - each - PASS)):
+            if 0 < t < STEPS:
+                here = (since >= 0) & (since % each == 0) & (since < chunks)
+
+                @pl.when(here & jnp.logical_not(edge))
+                def _():
+                    pass_copy(t, since // each, True).wait_recv()
+                    pass_copy(t, since // each).start()
+
     def both(copy, *where):
         return [copy(*(where[:1] + (side,) + where[1:])) for side in (LOW, HIGH)]
 
@@ -189,13 +237,13 @@
                 barrier, inc=1, device_id=partner, device_id_type=pl.DeviceIdType.MESH
             )
 
-    greet((*lat_at, *lon_at, lev_at[0]))
+    greet((*lat_at, *lon_at, lev_at[0], aslant))
 
     @pl.when(edge)
     def _():
         greet((across, turned, lifted))
 
-    pl.semaphore_wait(barrier, jnp.where(edge, 8, 5))
+    pl.semaphore_wait(barrier, jnp.where(edge, 9, 6))
 
     for copy in both(lon_copy, 0):
         copy.start()
@@ -277,6 +325,7 @@
 
         def chunk(n, carry, s=s):
             relays(s, n)
+            pass_on(s, n)
             for copy in both(lat_copy, s, n):
                 copy.wait_recv()
 
@@ -300,8 +349,7 @@
             @pl.when(n == 0)
             def _():
                 if s > 0:
-                    for copy in both(lev_copy, s, GROUPS - 1):
-                        copy.start()
+                    lev_start(s, GROUPS - 1)
                     for copy in both(lon_copy, s - 1):
                         copy.wait_send()
                 for copy in both(lon_copy, s):
@@ -322,8 +370,7 @@
 
                     @pl.when(n > 0)
                     def _():
-                        for copy in both(lev_copy, s + 1, n // each - 1):
-                            copy.start()
+                        lev_start(s + 1, n // each - 1)
 
             def row(r, inner):
                 new_row(s, n, r)
@@ -345,6 +392,12 @@
             for copy in both(lev_copy, t, group):
                 copy.wait_send()
     lax.fori_loop(0, chunks, drain, 0)
+
+    @pl.when(jnp.logical_not(edge))
+    def _():
+        for t in range(1, STEPS):
+            for group in range(GROUPS):
+                pass_copy(t, group).wait_send()
 
     for stage, there in enumerate((edge, corner)):
 
@@ -375,6 +428,7 @@
             pltpu.VMEM(faces, jnp.float32),
             pltpu.VMEM(faces, jnp.float32),
             pltpu.VMEM((2, width, tall, lanes), jnp.float32),
+            pltpu.VMEM((STEPS, width, depth, lanes), jnp.float32),
             dma((2,)),
             dma((2, chunks)),
             dma((2, 2, chunks)),
@@ -384,6 +438,8 @@
             dma((STEPS, 2, GROUPS)),
             dma((2, chunks)),
             dma((2, chunks)),
+            dma((STEPS, GROUPS)),
+            dma((STEPS, GROUPS)),
         ],
         compiler_params=pltpu.CompilerParams(
             collective_id=0, has_side_effects=True, vmem_limit_bytes=46 * 1024 * 1024

time: 243 us -> 240 us (0.988)
  Pallas kernels: 238 us -> 235 us
    pallas_call x1, Pallas kernels: 238 us -> 235 us  [local(): pl.pallas_call(kernel, out_shape=pltpu.VMEM(field.shape, field.dtype), in...]
where the time goes in v4:
time: 240 us
  Pallas kernels  235 us (98%)
  local copies, waits for them, and re-layouts  4.78 us (2%)
    pallas_call x1, Pallas kernels, local(): pl.pallas_call(kernel, out_shape=pltpu.VMEM(field.shape, field.dtype), in...  235 us

profile of v4, /device:TPU:16, one launch (start us, length us, event | category | flops | bytes accessed | tf_op | source)
XLA Modules:
  0.0 239.8 jit_solution(3506096022638914050)
XLA Ops:
  0.0 235.0 %march.1 = f32[4,64,96,128]{3,2,1,0:T(8,128)S(1)} custom-call(f32[4,64,96,128]{3,2,1,0:T(8,128)} %field.1, f32[4,64,96,128]{3,2,1,0:T(8,128)} %crowding.1), custom_call_target="tpu_custom_call" | custom-call | tf_op jit(solution)/shard_map/march/pallas_call | solution.py:419
  235.1 4.8 %copy.4 = f32[4,64,96,128]{3,2,1,0:T(8,128)} copy(f32[4,64,96,128]{3,2,1,0:T(8,128)S(1)} %march.1) | data formatting | bytes 25165824

commit v5 on v4

--- a/solution.py
+++ b/solution.py
@@ -12,7 +12,6 @@
 AHEAD = 10
 LEADS = (4, 2)
 SETTLE = 6
-DIRECT = 32
 PASS = 10
 GROUPS = 4
 LOW, HIGH = 0, 1
@@ -46,6 +45,11 @@
     across = {"lat": jnp.where(first, lat + 3, jnp.where(last, lat - 3, lat))}
     turned = {"lat": jnp.where(y == 0, lat + 4, lat - 4)}
     lifted = {"lat": lax.rem(lat + 8, 16)}
+    onward = {"lat": jnp.where(corner, lifted["lat"], turned["lat"])}
+
+    def held(stage, n):
+        return edge if stage == 0 else edge & (n % 2 == jnp.where(corner, 0, 1))
+
 
     inside = lat + jnp.where(x % 2 == 0, 1, -1)
     aslant = {"lat": inside, **beside("lev", 1)}
@@ -76,9 +80,6 @@
     def lat_start(t, side, n):
         plain = lat_copy(t, side, n)
         leaves = last if side == LOW else first
-        if t == STEPS - 1:
-            leaves = leaves & (n < DIRECT)
-
         @pl.when(leaves)
         def _():
             pltpu.make_async_remote_copy(
@@ -94,14 +95,14 @@
         def _():
             plain.start()
 
-    def relay_copy(t, stage, n, arrives):
+    def relay_copy(t, stage, n, arrives, target=None):
         rows = pl.ds(chunk_at(n) * ROWS, ROWS)
         return pltpu.make_async_remote_copy(
             src_ref=relay.at[stage, rows],
             dst_ref=lat_halo.at[t % 2, mine, rows] if arrives else relay.at[1, rows],
             send_sem=relay_send.at[stage, n],
             recv_sem=lat_recv.at[t % 2, mine, n] if arrives else relay_recv.at[1, n],
-            device_id=lifted if stage else turned,
+            device_id=target or (onward if stage else turned),
             device_id_type=pl.DeviceIdType.MESH,
         )
 
@@ -126,29 +127,33 @@
         def _():
             relay_copy(t, stage, n, True).start()
 
-        @pl.when(jnp.logical_not(corner))
-        def _():
-            relay_copy(t, stage, n, False).start()
+        @pl.when(jnp.logical_not(corner) & (n % 2 == 0))
+        def _():
+            relay_copy(t, stage, n, False, turned).start()
+
+        @pl.when(jnp.logical_not(corner) & (n % 2 == 1))
+        def _():
+            relay_copy(t, stage, n, False, lifted).start()
 
     def relays(s, n):
-        for stage, (lead, there) in enumerate(zip(LEADS, (edge, corner))):
+        for stage, lead in enumerate(LEADS):
             ahead = n + lead
-            here = there & (ahead < (DIRECT if s == STEPS - 1 else chunks))
+            there = held(stage, ahead)
+            here = there & (ahead < chunks)
 
             @pl.when(here)
             def _():
                 send_on(s, stage, ahead)
 
             if s < STEPS - 1:
-                end = DIRECT if s + 1 == STEPS - 1 else chunks
-
-                @pl.when(there & (ahead >= chunks) & (ahead - chunks < end))
+                @pl.when(there & (ahead >= chunks))
                 def _():
                     send_on(s + 1, stage, ahead - chunks)
 
             left = n - SETTLE
-
-            @pl.when(there & (left >= 0) & (left < (DIRECT if s == STEPS - 1 else chunks)))
+            there = held(stage, left + chunks)
+
+            @pl.when(there & (left >= 0))
             def _():
                 relay_copy(s, stage, left, True).wait_send()
 
@@ -270,15 +275,16 @@
             copy.start()
     load_crowd.wait()
 
-    for stage, (lead, there) in enumerate(zip(LEADS, (edge, corner))):
-
-        @pl.when(there)
-        def _(stage=stage, lead=lead):
-            def begin(n, carry):
+    for stage, lead in enumerate(LEADS):
+
+        def begin(n, carry, stage=stage):
+            @pl.when(held(stage, n))
+            def _():
                 send_on(0, stage, n)
-                return carry
-
-            lax.fori_loop(0, lead, begin, 0)
+
+            return carry
+
+        lax.fori_loop(0, lead, begin, 0)
 
     place = lax.broadcasted_iota(jnp.int32, (8, 128), 0)
 
@@ -399,15 +405,16 @@
             for group in range(GROUPS):
                 pass_copy(t, group).wait_send()
 
-    for stage, there in enumerate((edge, corner)):
-
-        @pl.when(there)
-        def _(stage=stage):
-            def settle(n, carry):
+    for stage in (0, 1):
+
+        def settle(n, carry, stage=stage):
+            @pl.when(held(stage, n))
+            def _():
                 relay_copy(STEPS - 1, stage, n, True).wait_send()
-                return carry
-
-            lax.fori_loop(chunks - SETTLE, DIRECT, settle, 0)
+
+            return carry
+
+        lax.fori_loop(chunks - SETTLE, chunks, settle, 0)
 
 
 def local(field, crowding):

time: 240 us -> 235 us (0.979)
  Pallas kernels: 235 us -> 230 us
    pallas_call x1, Pallas kernels: 235 us -> 230 us  [local(): pl.pallas_call(kernel, out_shape=pltpu.VMEM(field.shape, field.dtype), in...]
where the time goes in v5:
time: 235 us
  Pallas kernels  230 us (98%)
  local copies, waits for them, and re-layouts  4.78 us (2%)
    pallas_call x1, Pallas kernels, local(): pl.pallas_call(kernel, out_shape=pltpu.VMEM(field.shape, field.dtype), in...  230 us
    unnamed x1, local copies, waits for them, and re-layouts  4.78 us

profile of v5, /device:TPU:16, one launch (start us, length us, event | category | flops | bytes accessed | tf_op | source)
XLA Modules:
  0.0 235.2 jit_solution(12106943719780711808)
XLA Ops:
  0.0 230.4 %march.1 = f32[4,64,96,128]{3,2,1,0:T(8,128)S(1)} custom-call(f32[4,64,96,128]{3,2,1,0:T(8,128)} %field.1, f32[4,64,96,128]{3,2,1,0:T(8,128)} %crowding.1), custom_call_target="tpu_custom_call" | custom-call | tf_op jit(solution)/shard_map/march/pallas_call | solution.py:426
  230.4 4.8 %copy.4 = f32[4,64,96,128]{3,2,1,0:T(8,128)} copy(f32[4,64,96,128]{3,2,1,0:T(8,128)S(1)} %march.1) | data formatting | bytes 25165824

commit v6 on v5

--- a/solution.py
+++ b/solution.py
@@ -13,7 +13,7 @@
 LEADS = (4, 2)
 SETTLE = 6
 PASS = 10
-GROUPS = 4
+GROUPS = 8
 LOW, HIGH = 0, 1
 
 

time: 235 us -> 236 us (level)
  no operation moved by 1% of the time
where the time goes in v6:
time: 236 us
  Pallas kernels  231 us (98%)
  local copies, waits for them, and re-layouts  4.78 us (2%)
    pallas_call x1, Pallas kernels, local(): pl.pallas_call(kernel, out_shape=pltpu.VMEM(field.shape, field.dtype), in...  231 us
    unnamed x1, local copies, waits for them, and re-layouts  4.78 us

profile of v6, /device:TPU:16, one launch (start us, length us, event | category | flops | bytes accessed | tf_op | source)
XLA Modules:
  0.0 235.5 jit_solution(10733067860198760536)
XLA Ops:
  0.0 230.7 %march.1 = f32[4,64,96,128]{3,2,1,0:T(8,128)S(1)} custom-call(f32[4,64,96,128]{3,2,1,0:T(8,128)} %field.1, f32[4,64,96,128]{3,2,1,0:T(8,128)} %crowding.1), custom_call_target="tpu_custom_call" | custom-call | tf_op jit(solution)/shard_map/march/pallas_call | solution.py:426
  230.8 4.8 %copy.4 = f32[4,64,96,128]{3,2,1,0:T(8,128)} copy(f32[4,64,96,128]{3,2,1,0:T(8,128)S(1)} %march.1) | data formatting | bytes 25165824
